TPU v7x, 32 devices: a whole 2x2x4 slice. The times are simulated.
32 devices in a mesh: gx: 8 (over z, x), gy: 4 (over y, core).
Axes of the slice: x: 2, y: 2, z: 4, core: 2. Of those that a mesh axis runs over, the one named last changes fastest.
Arguments:
- source_tiles: bfloat16 [96, 32, 192, 384], P(('gx', 'gy')), may hold values from -6 to 6
- tile_offsets: int32 [2, 96], P(None, ('gx', 'gy')), may hold values from -128 to 896, as said below
- tile_shifts: int32 [96], P(('gx', 'gy')), may hold values from 0 to 63
- tile_counts: int32 [32], P(('gx', 'gy')), may hold values from 1 to 3, as said below
Outputs:
- merged_slab: float32 [32, 1024, 1024], P(None, 'gx', 'gy')
Inputs may be any that keep to these rules, and one draw needn't show every extreme that they name: `tile_offsets`: slot k belongs to the device of joined gx+gy index d = k // 3, that is gx index d // 4 and gy index d % 4. Its x offset lies from that gx index times 128 minus 64 up to that gx index times 128; its y offset from the gy index times 256 minus 128 up to the gy index times 256. So every tile covers its owner's whole block. `tile_counts`: entry d counts the used slots of device d; they are its first slots, the others are ignored. Both 1 and 3 occur in every draw.
All inputs are finite; a program needn't handle non-finite values.
Results may differ from a plain program's by a relative error of at most 0.0003.
Values sent between devices are 32-bit elements; how exact they have to be, the bound alone decides.
A program may use at most 192 MiB of HBM per device.

v0:
```python
import functools

import jax
import jax.numpy as jnp
from jax import lax
from jax.experimental import pallas as pl
from jax.experimental.pallas import tpu as pltpu
from jax.sharding import PartitionSpec as P

BX = 128
BY = 256
RAMP = 32
RX = 64
RY = 128
LAG_Y = 1
LAG_RELAY = 5
LAG_X = 12
LANES = 128
MESH = pl.DeviceIdType.MESH


def ramp_at(place, length):
    place = place.astype(jnp.float32)
    ramp = jnp.minimum(jnp.minimum(place + 1.0, length - place), float(RAMP))
    return jnp.maximum(ramp, 0.0)


def whole_iota(shape, dimension):
    return lax.broadcasted_iota(jnp.int32, shape, dimension)


def pick(index, options):
    chosen = options[-1]
    for number in range(len(options) - 2, -1, -1):
        chosen = jnp.where(index == number, options[number], chosen)
    return chosen


def kernel(
    grid_x, grid_y, offsets_ref, shifts_ref, counts_ref, first_ref, next_ref,
    out_ref, centre, up, down, above, below, from_left, from_right, relay, places,
    across, along, held, parts, scale,
    up_sent, down_sent, left_sent, right_sent, above_sem, below_sem, from_left_sem, from_right_sem,
    relay_sent, relay_sem, place_sent, place_sem,
):
    slots, length, rows = first_ref.shape[0], first_ref.shape[2], first_ref.shape[3]
    extent_x, extent_y = across.shape[0], along.shape[2]
    half = extent_y // 2
    count = centre.shape[0]
    pairs = grid_x // 2
    step = pl.program_id(0)
    column, row = lax.axis_index("gx"), lax.axis_index("gy")
    even = column % 2 == 0
    pair = column // 2
    has_left, has_right = column > 0, column < grid_x - 1
    has_below, has_above = row > 0, row < grid_y - 1
    far_left, far_right = column > 1, column < grid_x - 2
    to_left, to_right = (column - 1, row), (column + 1, row)
    to_below, to_above = (column, row - 1), (column, row + 1)
    to_far_left, to_far_right = (column - 2, row), (column + 2, row)

    def remote(source, target, sent, arrived, device):
        return pltpu.make_async_remote_copy(
            src_ref=source, dst_ref=target, send_sem=sent, recv_sem=arrived,
            device_id=device, device_id_type=MESH,
        )

    def copy_below(n):
        return remote(up.at[n], above.at[n], up_sent.at[n], above_sem.at[n], to_below)

    def copy_above(n):
        return remote(down.at[n], below.at[n], down_sent.at[n], below_sem.at[n], to_above)

    left_strip, right_strip = pl.ds(0, RX), pl.ds(RX + BX, RX)

    def copy_left(n):
        return remote(
            centre.at[n, left_strip], from_right.at[n], left_sent.at[n], from_right_sem.at[n], to_left
        )

    def copy_right(n):
        return remote(
            centre.at[n, right_strip], from_left.at[n], right_sent.at[n], from_left_sem.at[n], to_right
        )

    def detour_left(n):
        return remote(
            centre.at[n, left_strip], relay.at[n], left_sent.at[n], relay_sem.at[n], to_right
        )

    def detour_right(n):
        return remote(
            centre.at[n, right_strip], relay.at[n], right_sent.at[n], relay_sem.at[n], to_left
        )

    def relay_left(n):
        return remote(relay.at[n], from_right.at[n], relay_sent.at[n], from_right_sem.at[n], to_far_left)

    def relay_right(n):
        return remote(relay.at[n], from_left.at[n], relay_sent.at[n], from_left_sem.at[n], to_far_right)

    def by_relay_right(n):
        return n % pairs < pairs - 1 - pair

    def by_relay_left(n):
        return n % pairs < pair

    def place_copy(first, size, target, number, device):
        return remote(
            places.at[pl.ds(first, size)], places.at[pl.ds(target, size)],
            place_sent.at[number], place_sem.at[number], device,
        )

    place_above = place_copy(0, 1, 1, 0, to_above)
    place_below = place_copy(0, 1, 2, 1, to_below)
    place_right = place_copy(0, 3, 3, 2, to_right)
    place_left = place_copy(0, 3, 6, 3, to_left)

    def along_rows(plane, k):
        low = jnp.dot(plane, along[k, :, :half], preferred_element_type=jnp.float32)
        cut = half - RY
        high = jnp.dot(plane[:, cut:], along[k, cut:, half:], preferred_element_type=jnp.float32)
        return low, high

    @pl.when(step == 0)
    def _():
        barrier = pltpu.get_barrier_semaphore()
        peers = (
            (has_left, to_left), (has_right, to_right), (has_below, to_below), (has_above, to_above),
            (far_left, to_far_left), (far_right, to_far_right),
        )
        for there, device in peers:
            @pl.when(there)
            def _():
                pl.semaphore_signal(barrier, inc=1, device_id=device, device_id_type=MESH)

        starts_x = [offsets_ref[0, k] - column * BX for k in range(slots)]
        starts_y = [offsets_ref[1, k] - row * BY for k in range(slots)]
        active = [jnp.where(k < counts_ref[0], 1.0, 0.0) for k in range(slots)]
        shape = places.shape[1:]
        lane, tile = whole_iota(shape, 1), whole_iota(shape, 0)
        record = jnp.zeros(shape, jnp.float32)
        for k in range(slots):
            values = (starts_x[k].astype(jnp.float32), starts_y[k].astype(jnp.float32), active[k])
            for place, value in enumerate(values):
                record = jnp.where((tile == k) & (lane == place), value, record)
        places[0] = record
        for number in range(1, places.shape[0]):
            there = (has_below, has_above, has_left, has_right)[
                number - 1 if number < 3 else number // 3 + 1
            ]

            @pl.when(jnp.logical_not(there))
            def _():
                places[number] = jnp.zeros(shape, jnp.float32)

        for k in range(slots):
            fraction = (shifts_ref[k] % 4).astype(jnp.float32) * 0.25
            target = whole_iota((1, extent_y), 1) - (starts_y[k] + RY)
            ramp = ramp_at(target, rows)
            source = whole_iota((rows, extent_y), 0)
            here = jnp.where(source == target, ramp * (1.0 - fraction), 0.0)
            after = jnp.where(
                source == jnp.minimum(target + 1, rows - 1), ramp * fraction, 0.0
            )
            along[k] = (here + after).astype(jnp.bfloat16)
        wide = 2 * slots * length
        number = whole_iota((1, wide), 1)
        part = number // length
        source = number - part * length
        part = part // 2
        fraction = pick(
            part, [(shifts_ref[k] // 4 % 4).astype(jnp.float32) * 0.25 for k in range(slots)]
        )
        weight = pick(part, active)
        target = whole_iota((extent_x, wide), 0) - pick(part, [start + RX for start in starts_x])
        here = jnp.where(source == target, 1.0 - fraction, 0.0)
        after = jnp.where(source == jnp.minimum(target + 1, length - 1), fraction, 0.0)
        across[...] = (ramp_at(target, length) * weight * (here + after)).astype(jnp.bfloat16)

        for k in range(slots):
            low, high = along_rows(first_ref[k, 0], k)
            held[k, :, :half] = low
            held[k, :, half:] = high
        pl.semaphore_wait(barrier, sum(jnp.where(there, 1, 0) for there, device in peers))

        @pl.when(has_above)
        def _():
            place_above.start()

        @pl.when(has_below)
        def _():
            place_below.start()

    @pl.when(step < count)
    def _():
        for k in range(slots):
            fraction = (shifts_ref[k] // 16 % 4).astype(jnp.float32) * 0.25
            for number, later in enumerate(along_rows(next_ref[k, 0], k)):
                lanes = slice(number * half, (number + 1) * half)
                mixed = held[k, :, lanes] * (1.0 - fraction) + later * fraction
                held[k, :, lanes] = later
                top = mixed.astype(jnp.bfloat16)
                rest = (mixed - top.astype(jnp.float32)).astype(jnp.bfloat16)
                parts[2 * k * length : (2 * k + 1) * length, lanes] = top
                parts[(2 * k + 1) * length : (2 * k + 2) * length, lanes] = rest
        total = jnp.dot(across[...], parts[...], preferred_element_type=jnp.float32)
        up[step] = total[:, :RY]
        centre[step] = total[:, RY : RY + BY]
        down[step] = total[:, RY + BY :]

        @pl.when(has_below)
        def _():
            copy_below(step).start()

        @pl.when(has_above)
        def _():
            copy_above(step).start()

    @pl.when(step == LAG_Y)
    def _():
        @pl.when(has_below)
        def _():
            place_above.wait_recv()

        @pl.when(has_above)
        def _():
            place_below.wait_recv()

        @pl.when(has_right)
        def _():
            place_right.start()

        @pl.when(has_left)
        def _():
            place_left.start()

    @pl.when((step >= LAG_Y) & (step < count + LAG_Y))
    def _():
        n = step - LAG_Y

        @pl.when(has_below)
        def _():
            copy_above(n).wait_recv()
            centre[n, :, :RY] += below[n]

        @pl.when(has_above)
        def _():
            copy_below(n).wait_recv()
            centre[n, :, RY:] += above[n]

        detours_left = even & by_relay_left(n)
        detours_right = jnp.logical_not(even) & by_relay_right(n)

        @pl.when(has_left & detours_left)
        def _():
            detour_left(n).start()

        @pl.when(has_left & jnp.logical_not(detours_left))
        def _():
            copy_left(n).start()

        @pl.when(has_right & detours_right)
        def _():
            detour_right(n).start()

        @pl.when(has_right & jnp.logical_not(detours_right))
        def _():
            copy_right(n).start()

    @pl.when((step >= LAG_RELAY) & (step < count + LAG_RELAY))
    def _():
        n = step - LAG_RELAY

        @pl.when(even & far_right & by_relay_right(n))
        def _():
            detour_right(n).wait_recv()
            relay_right(n).start()

        @pl.when(jnp.logical_not(even) & far_left & by_relay_left(n))
        def _():
            detour_left(n).wait_recv()
            relay_left(n).start()

    @pl.when(step == LAG_X)
    def _():
        for there, copy in ((has_above, place_above), (has_below, place_below)):
            @pl.when(there)
            def _():
                copy.wait_send()

        @pl.when(has_left)
        def _():
            place_right.wait_recv()
            place_left.wait_send()

        @pl.when(has_right)
        def _():
            place_left.wait_recv()
            place_right.wait_send()

        total = jnp.zeros((BX, BY), jnp.float32)
        cell_x = whole_iota((BX, 1), 0).astype(jnp.float32)
        cell_y = whole_iota((1, BY), 1).astype(jnp.float32)
        for number in range(places.shape[0]):
            origin_x = float((0, -BX, BX)[number // 3])
            origin_y = float((0, -BY, BY)[number % 3])
            for k in range(slots):
                start_x = places[number, k : k + 1, 0:1] + origin_x
                start_y = places[number, k : k + 1, 1:2] + origin_y
                weight = places[number, k : k + 1, 2:3]
                total += (ramp_at(cell_x - start_x, length) * weight) * ramp_at(cell_y - start_y, rows)
        scale[...] = 1.0 / jnp.maximum(total, 1.0)

    @pl.when(step >= LAG_X)
    def _():
        n = step - LAG_X

        @pl.when(has_left)
        def _():
            copy_right(n).wait_recv()
            centre[n, RX : 2 * RX] += from_left[n]
            copy_left(n).wait_send()

        @pl.when(has_right)
        def _():
            copy_left(n).wait_recv()
            centre[n, BX : BX + RX] += from_right[n]
            copy_right(n).wait_send()

        @pl.when(has_below)
        def _():
            copy_below(n).wait_send()

        @pl.when(has_above)
        def _():
            copy_above(n).wait_send()

        @pl.when(even & far_right & by_relay_right(n))
        def _():
            relay_right(n).wait_send()

        @pl.when(jnp.logical_not(even) & far_left & by_relay_left(n))
        def _():
            relay_left(n).wait_send()

        out_ref[n] = centre[n, RX : RX + BX] * scale[...]


def local(grid_x, grid_y, tiles, tile_offsets, tile_shifts, tile_counts):
    slots, count, length, rows = tiles.shape
    extent_x, extent_y = BX + 2 * RX, BY + 2 * RY
    plane = (slots, 1, length, rows)
    slab = lambda *shape: pltpu.VMEM((count,) + shape, jnp.float32)
    return pl.pallas_call(
        functools.partial(kernel, grid_x, grid_y),
        grid=(count + LAG_X,),
        in_specs=[
            pl.BlockSpec(memory_space=pltpu.SMEM),
            pl.BlockSpec(memory_space=pltpu.SMEM),
            pl.BlockSpec(memory_space=pltpu.SMEM),
            pl.BlockSpec(plane, lambda s: (0, 0, 0, 0)),
            pl.BlockSpec(plane, lambda s: (0, jnp.minimum(s + 1, count - 1), 0, 0)),
        ],
        out_specs=pl.BlockSpec(memory_space=pltpu.VMEM),
        out_shape=pltpu.VMEM((count, BX, BY), jnp.float32),
        scratch_shapes=[
            slab(extent_x, BY),
            slab(extent_x, RY),
            slab(extent_x, RY),
            slab(extent_x, RY),
            slab(extent_x, RY),
            slab(RX, BY),
            slab(RX, BY),
            slab(RX, BY),
            pltpu.VMEM((9, 8 * pl.cdiv(slots, 8), LANES), jnp.float32),
            pltpu.VMEM((extent_x, 2 * slots * length), jnp.bfloat16),
            pltpu.VMEM((slots, rows, extent_y), jnp.bfloat16),
            pltpu.VMEM((slots, length, extent_y), jnp.float32),
            pltpu.VMEM((2 * slots * length, extent_y), jnp.bfloat16),
            pltpu.VMEM((BX, BY), jnp.float32),
        ]
        + [pltpu.SemaphoreType.DMA((count,))] * 10
        + [pltpu.SemaphoreType.DMA((4,))] * 2,
        compiler_params=pltpu.CompilerParams(
            collective_id=0, has_side_effects=True, vmem_limit_bytes=52 * 1024 * 1024,
            dimension_semantics=("arbitrary",),
        ),
        name="merged",
    )(tile_offsets, tile_shifts, tile_counts, tiles, tiles)


def solution(mesh):
    placed = (
        P(("gx", "gy"), None, None, None),
        P(None, ("gx", "gy")),
        P(("gx", "gy")),
        P(("gx", "gy")),
    )
    return jax.shard_map(
        functools.partial(local, mesh.shape["gx"], mesh.shape["gy"]),
        mesh=mesh, in_specs=placed, out_specs=P(None, "gx", "gy"), check_vma=False,
    )
```

profile of v0, /device:TPU:1, one launch (start us, length us, event | category | flops | bytes accessed | tf_op | source)
XLA Modules:
  0.0 93.8 jit_solution(6214970578718407796)
XLA Ops:
  0.7 91.1 %merged.1 = f32[32,128,256]{2,1,0:T(8,128)S(1)} custom-call(s32[2,3]{1,0:T(2,128)} %offsets_ref.1, s32[3]{0:T(128)} %shifts_ref.1, s32[1]{0:T(128)S(6)} %copy.7.counts_ref, bf16[3,32,192,384]{3,2,1,0:T(8,128)(2,1)} %next_ref.1, bf16[3,32,192,384]{3,2,1,0:T(8,128)(2,1)} %next_ref.1), custom_call_target="tpu_custom_call" | custom-call | tf_op jit(solution)/shard_map/merged/pallas_call | solution.py:355
  91.8 2.0 %copy.6 = f32[32,128,256]{2,1,0:T(8,128)} copy(f32[32,128,256]{2,1,0:T(8,128)S(1)} %merged.1) | data formatting | bytes 8388608
where the time goes:
time: 94.2 us; the launch traced here: 93.8 us
  Pallas kernels  91.1 us (97%)
  local copies, waits for them, and re-layouts  2.02 us (2%)
    pallas_call x1, Pallas kernels, local(): pl.pallas_call(functools.partial(kernel, grid_x, grid_y), grid=(count + L...  91.1 us
    unnamed x1, local copies, waits for them, and re-layouts  2.02 us

commit v1 on v0

v1 whole, which is shorter than its diff:
```python
import functools

import jax
import jax.numpy as jnp
from jax import lax
from jax.experimental import pallas as pl
from jax.experimental.pallas import tpu as pltpu
from jax.sharding import PartitionSpec as P

BX = 128
BY = 256
RAMP = 32
RX = 64
RY = 128
RING = 4
GROUP = 4
HEAD = 8
FIRST = ((0, 1), (1, 1), (2, 1), (3, 1), (4, 2), (6, 2))
TURNS = 4
FIRST_TURN = ((0, 2), (1, 3), (2, 0), (3, 1), (0, 2), (1, 3))
GROUP_TURN = ((0, 2), (1, 3), (0, 2), (1, 0), (1, 2), (3, 3))
FLIGHT = 8
LAG_NEAR = 1
LAG_FAR = 3
LAG_PLACE = 2
LANES = 128
MESH = pl.DeviceIdType.MESH


def ramp_at(place, length):
    place = place.astype(jnp.float32)
    ramp = jnp.minimum(jnp.minimum(place + 1.0, length - place), float(RAMP))
    return jnp.maximum(ramp, 0.0)


def whole_iota(shape, dimension):
    return lax.broadcasted_iota(jnp.int32, shape, dimension)


def pick(index, options):
    chosen = options[-1]
    for number in range(len(options) - 2, -1, -1):
        chosen = jnp.where(index == number, options[number], chosen)
    return chosen


def kernel(
    grid_x, grid_y, offsets_hbm, shifts_hbm, counts_hbm, tiles_ref, out_ref,
    offsets_ref, shifts_ref, counts_ref,
    planes, strips, arrived, relay, edges, edges_in, middles, middles_in, places,
    across, along, held, parts, scale,
    small_sem, plane_sem, strip_sent, strip_sem, relay_sent, relay_sem,
    edge_sent, edge_sem, middle_sent, middle_sem, place_sent, place_sem,
):
    slots, count, length, rows = tiles_ref.shape
    extent_x, extent_y = across.shape[0], along.shape[2]
    half = extent_y // 2
    groups = count // GROUP
    pairs = grid_x // 2
    column, row = lax.axis_index("gx"), lax.axis_index("gy")
    even = column % 2 == 0
    pair = column // 2
    has_left, has_right = column > 0, column < grid_x - 1
    has_below, has_above = row > 0, row < grid_y - 1
    far_left, far_right = column > 1, column < grid_x - 2
    to_left, to_right = (column - 1, row), (column + 1, row)
    to_below, to_above = (column, row - 1), (column, row + 1)
    to_far_left, to_far_right = (column - 2, row), (column + 2, row)
    odd_row = row % 2 == 1
    near, far = (row + 1) % 2, row % 2
    has_near = (odd_row & has_below) | (jnp.logical_not(odd_row) & has_above)
    has_far = (odd_row & has_above) | (jnp.logical_not(odd_row) & has_below)

    def remote(source, target, sent, done, device):
        return pltpu.make_async_remote_copy(
            src_ref=source, dst_ref=target, send_sem=sent, recv_sem=done,
            device_id=device, device_id_type=MESH,
        )

    def fetch(n):
        slot = n % RING
        return pltpu.make_async_copy(tiles_ref.at[:, n], planes.at[slot], plane_sem.at[slot])

    def edge_below(n):
        return remote(
            edges.at[0, n], edges_in.at[1, n], edge_sent.at[0], edge_sem.at[1, n % FLIGHT], to_below
        )

    def edge_above(n):
        return remote(
            edges.at[1, n], edges_in.at[0, n], edge_sent.at[1], edge_sem.at[0, n % FLIGHT], to_above
        )

    def whole_edges(side, device):
        return remote(
            edges.at[side], edges_in.at[1 - side], edge_sent.at[side], edge_sem.at[1 - side, 0], device
        )

    def middle(side, device):
        return remote(
            middles.at[side], middles_in.at[1 - side], middle_sent.at[side], middle_sem.at[1 - side], device
        )

    def stage_of(start):
        return start // HEAD

    def strip(side, unit, part, device):
        number, start, size, turns = unit
        span = pl.ds(start, size)
        return remote(
            strips.at[side, part, span], arrived.at[1 - side, span, part],
            strip_sent.at[side], strip_sem.at[1 - side, stage_of(start)], device,
        )

    def whole_stage(side, stage):
        span = pl.ds(stage * HEAD, HEAD)
        return remote(
            arrived.at[side, span], arrived.at[side, span],
            strip_sent.at[side], strip_sem.at[side, stage], to_left,
        )

    def whole_strips(side, device):
        return remote(
            strips.at[side], strips.at[side], strip_sent.at[side], strip_sem.at[side, 0], device
        )

    def detour(side, unit, part, device):
        number, start, size, turns = unit
        span = pl.ds(start, size)
        return remote(
            strips.at[side, part, span], relay.at[part, span],
            strip_sent.at[side], relay_sem.at[part, number], device,
        )

    def onward(side, unit, part, device):
        number, start, size, turns = unit
        span = pl.ds(start, size)
        return remote(
            relay.at[part, span], arrived.at[1 - side, span, part],
            relay_sent.at[part, number], strip_sem.at[1 - side, stage_of(start)], device,
        )

    def turn(unit, part):
        lower, upper = unit[3]
        return jnp.where(part == 0, lower, upper)

    def by_relay_left(unit, part):
        return turn(unit, part) * pairs < TURNS * pair

    def by_relay_right(unit, part):
        return turn(unit, part) * pairs < TURNS * (pairs - 1 - pair)

    def send_unit(unit, part):
        turns_left = even & by_relay_left(unit, part)
        turns_right = jnp.logical_not(even) & by_relay_right(unit, part)

        @pl.when(has_left & turns_left)
        def _():
            detour(0, unit, part, to_right).start()

        @pl.when(has_left & jnp.logical_not(turns_left))
        def _():
            strip(0, unit, part, to_left).start()

        @pl.when(has_right & turns_right)
        def _():
            detour(1, unit, part, to_left).start()

        @pl.when(has_right & jnp.logical_not(turns_right))
        def _():
            strip(1, unit, part, to_right).start()

    first_units = [
        (number, start, size, FIRST_TURN[number]) for number, (start, size) in enumerate(FIRST)
    ]

    def group_unit(g):
        kinds = len(GROUP_TURN)
        place = (g - HEAD // GROUP) % kinds
        turns = tuple(pick(place, [GROUP_TURN[i][part] for i in range(kinds)]) for part in (0, 1))
        return len(FIRST) - HEAD // GROUP + g, g * GROUP, GROUP, turns

    def relays_right(unit, part):
        return even & far_right & by_relay_right(unit, part)

    def relays_left(unit, part):
        return jnp.logical_not(even) & far_left & by_relay_left(unit, part)

    def relay_unit(unit):
        for part in (near, far):
            @pl.when(relays_right(unit, part))
            def _():
                detour(1, unit, part, to_left).wait_recv()
                onward(1, unit, part, to_far_right).start()

            @pl.when(relays_left(unit, part))
            def _():
                detour(0, unit, part, to_right).wait_recv()
                onward(0, unit, part, to_far_left).start()

    def relay_done(unit):
        for part in (0, 1):
            @pl.when(relays_right(unit, part))
            def _():
                onward(1, unit, part, to_far_right).wait_send()

            @pl.when(relays_left(unit, part))
            def _():
                onward(0, unit, part, to_far_left).wait_send()

    def place_copy(first, size, target, number, device):
        return remote(
            places.at[pl.ds(first, size)], places.at[pl.ds(target, size)],
            place_sent.at[number], place_sem.at[number], device,
        )

    place_above = place_copy(0, 1, 1, 0, to_above)
    place_below = place_copy(0, 1, 2, 1, to_below)
    place_right = place_copy(0, 3, 3, 2, to_right)
    place_left = place_copy(0, 3, 6, 3, to_left)

    def along_rows(slot, k):
        plane = planes[slot, k]
        low = jnp.dot(plane, along[k, :, :half], preferred_element_type=jnp.float32)
        cut = half - RY
        high = jnp.dot(plane[:, cut:], along[k, cut:, half:], preferred_element_type=jnp.float32)
        return low, high

    small = [
        pltpu.make_async_copy(source, target, small_sem.at[number])
        for number, (source, target) in enumerate(
            ((offsets_hbm, offsets_ref), (shifts_hbm, shifts_ref), (counts_hbm, counts_ref))
        )
    ]
    for copy in small:
        copy.start()
    barrier = pltpu.get_barrier_semaphore()
    peers = (
        (has_left, to_left), (has_right, to_right), (has_below, to_below), (has_above, to_above),
        (far_left, to_far_left), (far_right, to_far_right),
    )
    for there, device in peers:
        @pl.when(there)
        def _():
            pl.semaphore_signal(barrier, inc=1, device_id=device, device_id_type=MESH)
    for n in range(RING):
        fetch(n).start()
    for copy in small:
        copy.wait()

    starts_x = [offsets_ref[0, k] - column * BX for k in range(slots)]
    starts_y = [offsets_ref[1, k] - row * BY for k in range(slots)]
    active = [jnp.where(k < counts_ref[0, 0], 1.0, 0.0) for k in range(slots)]
    shape = places.shape[1:]
    lane, tile = whole_iota(shape, 1), whole_iota(shape, 0)
    record = jnp.zeros(shape, jnp.float32)
    for k in range(slots):
        values = (starts_x[k].astype(jnp.float32), starts_y[k].astype(jnp.float32), active[k])
        for place, value in enumerate(values):
            record = jnp.where((tile == k) & (lane == place), value, record)
    places[0] = record
    for number in range(1, places.shape[0]):
        there = (has_below, has_above, has_left, has_right)[
            number - 1 if number < 3 else number // 3 + 1
        ]

        @pl.when(jnp.logical_not(there))
        def _():
            places[number] = jnp.zeros(shape, jnp.float32)

    for k in range(slots):
        fraction = (shifts_ref[k] % 4).astype(jnp.float32) * 0.25
        target = whole_iota((1, extent_y), 1) - (starts_y[k] + RY)
        ramp = ramp_at(target, rows)
        here = jnp.where(target == rows - 1, ramp, ramp * (1.0 - fraction))
        after = ramp * fraction
        for first, lanes in ((0, slice(0, half)), (half - RY, slice(half, extent_y))):
            source = whole_iota((rows - first, half), 0) + first
            blend = jnp.where(
                source == target[:, lanes], here[:, lanes],
                jnp.where(source == target[:, lanes] + 1, after[:, lanes], 0.0),
            )
            along[k, first:, lanes] = blend.astype(jnp.bfloat16)
    wide = 2 * slots * length
    number = whole_iota((1, wide), 1)
    part = number // length
    source = number - part * length
    part = part // 2
    fraction = pick(
        part, [(shifts_ref[k] // 4 % 4).astype(jnp.float32) * 0.25 for k in range(slots)]
    )
    weight = pick(part, active)
    ramp = ramp_at(source, length) * weight
    here = jnp.where(source == length - 1, ramp, ramp * (1.0 - fraction))
    after = ramp_at(source - 1, length) * weight * fraction
    target = source + pick(part, [start + RX for start in starts_x])
    cell = whole_iota((extent_x, wide), 0)
    blend = jnp.where(cell == target, here, jnp.where(cell == target - 1, after, 0.0))
    across[...] = blend.astype(jnp.bfloat16)

    fetch(0).wait()
    for k in range(slots):
        low, high = along_rows(0, k)
        held[k, :, :half] = low
        held[k, :, half:] = high
    fetch(RING).start()

    def merge(n, part, there):
        @pl.when((n >= 0) & (n < count))
        def _():
            @pl.when(there & (part == 0))
            def _():
                edge_above(n).wait_recv()

            @pl.when(there & (part == 1))
            def _():
                edge_below(n).wait_recv()

            @pl.when(there)
            def _():
                strips[0, part, n] += edges_in[part, n, :RX]
                strips[1, part, n] += edges_in[part, n, RX:]

            for unit in first_units:
                @pl.when(n == unit[1] + unit[2] - 1)
                def _():
                    send_unit(unit, part)

            @pl.when((n >= HEAD) & (n % GROUP == GROUP - 1))
            def _():
                send_unit(group_unit(n // GROUP), part)

    lag_near = jnp.where(has_near, LAG_NEAR, 0)
    lag_far = jnp.where(has_far, LAG_FAR, 0)

    def step(s, carry):
        @pl.when(s < count)
        def _():
            @pl.when(s < count - 1)
            def _():
                fetch(s + 1).wait()

            slot = jnp.minimum(s + 1, count - 1) % RING
            for k in range(slots):
                fraction = (shifts_ref[k] // 16 % 4).astype(jnp.float32) * 0.25
                for number, later in enumerate(along_rows(slot, k)):
                    lanes = slice(number * half, (number + 1) * half)
                    mixed = held[k, :, lanes] * (1.0 - fraction) + later * fraction
                    held[k, :, lanes] = later
                    top = mixed.astype(jnp.bfloat16)
                    rest = (mixed - top.astype(jnp.float32)).astype(jnp.bfloat16)
                    parts[2 * k * length : (2 * k + 1) * length, lanes] = top
                    parts[(2 * k + 1) * length : (2 * k + 2) * length, lanes] = rest

            @pl.when(s + 1 + RING < count)
            def _():
                fetch(s + 1 + RING).start()

            total = jnp.dot(across[...], parts[...], preferred_element_type=jnp.float32)
            left, centre, right = total[:RX], total[RX : RX + BX], total[RX + BX :]
            edges[0, s, :RX] = left[:, :RY]
            edges[0, s, RX:] = right[:, :RY]
            edges[1, s, :RX] = left[:, RY + BY :]
            edges[1, s, RX:] = right[:, RY + BY :]
            for part in (0, 1):
                strips[0, part, s] = left[:, (part + 1) * RY : (part + 2) * RY]
                strips[1, part, s] = right[:, (part + 1) * RY : (part + 2) * RY]

            @pl.when(s == 0)
            def _():
                pl.semaphore_wait(barrier, sum(jnp.where(there, 1, 0) for there, device in peers))

                @pl.when(has_above)
                def _():
                    place_above.start()

                @pl.when(has_below)
                def _():
                    place_below.start()

            @pl.when(has_below)
            def _():
                edge_below(s).start()

            @pl.when(has_above)
            def _():
                edge_above(s).start()

            middles[0, s] = centre[:, :RY]
            middles[1, s] = centre[:, RY + BY :]
            out_ref[s] = centre[:, RY : RY + BY]

        merge(s - lag_near, near, has_near)
        merge(s - lag_far, far, has_far)

        @pl.when(s == LAG_PLACE)
        def _():
            @pl.when(has_below)
            def _():
                place_above.wait_recv()

            @pl.when(has_above)
            def _():
                place_below.wait_recv()

            @pl.when(has_right)
            def _():
                place_right.start()

            @pl.when(has_left)
            def _():
                place_left.start()

        return carry

    lax.fori_loop(0, count + max(LAG_NEAR, LAG_FAR), step, 0)

    @pl.when(has_below)
    def _():
        middle(0, to_below).start()

    @pl.when(has_above)
    def _():
        middle(1, to_above).start()

    for there, copy in ((has_above, place_above), (has_below, place_below)):
        @pl.when(there)
        def _():
            copy.wait_send()

    @pl.when(has_left)
    def _():
        place_right.wait_recv()
        place_left.wait_send()

    @pl.when(has_right)
    def _():
        place_left.wait_recv()
        place_right.wait_send()

    total = jnp.zeros((BX, BY), jnp.float32)
    cell_x = whole_iota((BX, 1), 0).astype(jnp.float32)
    cell_y = whole_iota((1, BY), 1).astype(jnp.float32)
    for number in range(places.shape[0]):
        origin_x = float((0, -BX, BX)[number // 3])
        origin_y = float((0, -BY, BY)[number % 3])
        for k in range(slots):
            start_x = places[number, k : k + 1, 0:1] + origin_x
            start_y = places[number, k : k + 1, 1:2] + origin_y
            weight = places[number, k : k + 1, 2:3]
            total += (ramp_at(cell_x - start_x, length) * weight) * ramp_at(cell_y - start_y, rows)
    scale[...] = 1.0 / jnp.maximum(total, 1.0)

    for unit in first_units:
        relay_unit(unit)

    def relay_group(g, carry):
        relay_unit(group_unit(g))
        return carry

    lax.fori_loop(HEAD // GROUP, groups, relay_group, 0)

    @pl.when(has_below)
    def _():
        whole_edges(0, to_below).wait_send()
        middle(0, to_below).wait_send()
        middle(1, to_above).wait_recv()

    @pl.when(has_above)
    def _():
        whole_edges(1, to_above).wait_send()
        middle(1, to_above).wait_send()
        middle(0, to_below).wait_recv()

    def finish_stage(stage, carry):
        @pl.when(has_left)
        def _():
            whole_stage(0, stage).wait_recv()

        @pl.when(has_right)
        def _():
            whole_stage(1, stage).wait_recv()

        def finish(i, carry):
            n = stage * HEAD + i

            @pl.when(has_below)
            def _():
                out_ref[n, :, :RY] += middles_in[0, n]

            @pl.when(has_above)
            def _():
                out_ref[n, :, RY:] += middles_in[1, n]

            for part in (0, 1):
                lanes = slice(part * RY, (part + 1) * RY)

                @pl.when(has_left)
                def _():
                    out_ref[n, :RX, lanes] += arrived[0, n, part]

                @pl.when(has_right)
                def _():
                    out_ref[n, BX - RX :, lanes] += arrived[1, n, part]

            out_ref[n] = out_ref[n] * scale[...]
            return carry

        lax.fori_loop(0, HEAD, finish, 0)
        return carry

    lax.fori_loop(0, count // HEAD, finish_stage, 0)

    @pl.when(has_left)
    def _():
        whole_strips(0, to_left).wait_send()

    @pl.when(has_right)
    def _():
        whole_strips(1, to_right).wait_send()

    for unit in first_units:
        relay_done(unit)

    def relay_group_done(g, carry):
        relay_done(group_unit(g))
        return carry

    lax.fori_loop(HEAD // GROUP, groups, relay_group_done, 0)


def local(grid_x, grid_y, tiles, tile_offsets, tile_shifts, tile_counts):
    slots, count, length, rows = tiles.shape
    extent_x, extent_y = BX + 2 * RX, BY + 2 * RY
    units = len(FIRST) + (count - HEAD) // GROUP
    vmem = lambda *shape: pltpu.VMEM(shape, jnp.float32)
    sems = lambda *shape: pltpu.SemaphoreType.DMA(shape)
    return pl.pallas_call(
        functools.partial(kernel, grid_x, grid_y),
        in_specs=[
            pl.BlockSpec(memory_space=pltpu.HBM),
            pl.BlockSpec(memory_space=pltpu.HBM),
            pl.BlockSpec(memory_space=pltpu.HBM),
            pl.BlockSpec(memory_space=pltpu.HBM),
        ],
        out_specs=pl.BlockSpec(memory_space=pltpu.VMEM),
        out_shape=pltpu.VMEM((count, BX, BY), jnp.float32),
        scratch_shapes=[
            pltpu.SMEM((2, slots), jnp.int32),
            pltpu.SMEM((slots,), jnp.int32),
            pltpu.SMEM((1, 1), jnp.int32),
            pltpu.VMEM((RING, slots, length, rows), jnp.bfloat16),
            vmem(2, 2, count, RX, RY),
            vmem(2, count, 2, RX, RY),
            vmem(2, count, RX, RY),
            vmem(2, count, 2 * RX, RY),
            vmem(2, count, 2 * RX, RY),
            vmem(2, count, BX, RY),
            vmem(2, count, BX, RY),
            vmem(9, 8 * pl.cdiv(slots, 8), LANES),
            pltpu.VMEM((extent_x, 2 * slots * length), jnp.bfloat16),
            pltpu.VMEM((slots, rows, extent_y), jnp.bfloat16),
            vmem(slots, length, extent_y),
            pltpu.VMEM((2 * slots * length, extent_y), jnp.bfloat16),
            vmem(BX, BY),
            sems(3), sems(RING),
            sems(2), sems(2, count // HEAD), sems(2, units), sems(2, units),
            sems(2), sems(2, FLIGHT),
            sems(2), sems(2),
            sems(4), sems(4),
        ],
        compiler_params=pltpu.CompilerParams(
            collective_id=0, has_side_effects=True, vmem_limit_bytes=52 * 1024 * 1024,
        ),
        name="merged",
    )(tile_offsets, tile_shifts, tile_counts.reshape(1, 1), tiles)


def solution(mesh):
    placed = (
        P(("gx", "gy"), None, None, None),
        P(None, ("gx", "gy")),
        P(("gx", "gy")),
        P(("gx", "gy")),
    )
    return jax.shard_map(
        functools.partial(local, mesh.shape["gx"], mesh.shape["gy"]),
        mesh=mesh, in_specs=placed, out_specs=P(None, "gx", "gy"), check_vma=False,
    )
```

time: 94.2 us -> 90.3 us (0.959)
  Pallas kernels: 91.1 us -> 87.3 us
    pallas_call x1, Pallas kernels: 91.1 us -> 87.3 us  [local(): pl.pallas_call(functools.partial(kernel, grid_x, grid_y), in_specs=[pl.Bl...]
where the time goes in v1:
time: 90.3 us; the launch traced here: 89.9 us
  Pallas kernels  87.3 us (97%)
  local copies, waits for them, and re-layouts  2.02 us (2%)
    pallas_call x1, Pallas kernels, local(): pl.pallas_call(functools.partial(kernel, grid_x, grid_y), in_specs=[pl.Bl...  87.3 us
    unnamed x1, local copies, waits for them, and re-layouts  2.02 us

profile of v1, /device:TPU:1, one launch (start us, length us, event | category | flops | bytes accessed | tf_op | source)
XLA Modules:
  0.0 89.9 jit_solution(2229905452928677865)
XLA Ops:
  0.7 87.3 %merged.1 = f32[32,128,256]{2,1,0:T(8,128)S(1)} custom-call(s32[2,3]{1,0:T(2,128)} %offsets_hbm.1, s32[3]{0:T(128)} %shifts_hbm.1, s32[1,1]{1,0:T(1,128)} %bitcast.1.counts_hbm, bf16[3,32,192,384]{3,2,1,0:T(8,128)(2,1)} %tiles_ref.1), custom_call_target="tpu_custom_call" | custom-call | tf_op jit(solution)/shard_map/merged/pallas_call | solution.py:538
  87.9 2.0 %copy.6 = f32[32,128,256]{2,1,0:T(8,128)} copy(f32[32,128,256]{2,1,0:T(8,128)S(1)} %merged.1) | data formatting | bytes 8388608

commit v2 on v1

--- a/solution.py
+++ b/solution.py
@@ -13,12 +13,10 @@
 RX = 64
 RY = 128
 RING = 4
-GROUP = 4
-HEAD = 8
-FIRST = ((0, 1), (1, 1), (2, 1), (3, 1), (4, 2), (6, 2))
+STEPS = (1, 2)
+LAST = 2
+STAGES = 4
 TURNS = 4
-FIRST_TURN = ((0, 2), (1, 3), (2, 0), (3, 1), (0, 2), (1, 3))
-GROUP_TURN = ((0, 2), (1, 3), (0, 2), (1, 0), (1, 2), (3, 3))
 FLIGHT = 8
 LAG_NEAR = 1
 LAG_FAR = 3
@@ -42,6 +40,30 @@
     for number in range(len(options) - 2, -1, -1):
         chosen = jnp.where(index == number, options[number], chosen)
     return chosen
+
+
+def cut(length, steps):
+    sizes = []
+    for size in steps:
+        if size <= length:
+            sizes.append(size)
+            length -= size
+    return sizes + [length] if length else sizes
+
+
+def units_of(count):
+    tail = count // TURNS
+    cuts = [
+        (size, turns)
+        for size in cut((count - tail) // 3, STEPS)
+        for turns in ((0, 1), (2, 0), (1, 2))
+    ]
+    cuts += [(size, (3, 3)) for size in cut(tail, (LAST,) * (tail // LAST))]
+    units, start = [], 0
+    for size, turns in cuts:
+        units.append((len(units), start, size, turns, max(0, len(units) - len(cuts) + STAGES)))
+        start += size
+    return units
 
 
 def kernel(
@@ -55,7 +77,7 @@
     slots, count, length, rows = tiles_ref.shape
     extent_x, extent_y = across.shape[0], along.shape[2]
     half = extent_y // 2
-    groups = count // GROUP
+    units = units_of(count)
     pairs = grid_x // 2
     column, row = lax.axis_index("gx"), lax.axis_index("gy")
     even = column % 2 == 0
@@ -79,7 +101,7 @@
 
     def fetch(n):
         slot = n % RING
-        return pltpu.make_async_copy(tiles_ref.at[:, n], planes.at[slot], plane_sem.at[slot])
+        return pltpu.make_async_copy(tiles_ref.at[:, n], planes.at[:, slot], plane_sem.at[slot])
 
     def edge_below(n):
         return remote(
@@ -101,19 +123,16 @@
             middles.at[side], middles_in.at[1 - side], middle_sent.at[side], middle_sem.at[1 - side], device
         )
 
-    def stage_of(start):
-        return start // HEAD
-
     def strip(side, unit, part, device):
-        number, start, size, turns = unit
+        number, start, size, turns, stage = unit
         span = pl.ds(start, size)
         return remote(
             strips.at[side, part, span], arrived.at[1 - side, span, part],
-            strip_sent.at[side], strip_sem.at[1 - side, stage_of(start)], device,
-        )
-
-    def whole_stage(side, stage):
-        span = pl.ds(stage * HEAD, HEAD)
+            strip_sent.at[side], strip_sem.at[1 - side, stage], device,
+        )
+
+    def whole_stage(side, stage, first, last):
+        span = pl.ds(first, last - first)
         return remote(
             arrived.at[side, span], arrived.at[side, span],
             strip_sent.at[side], strip_sem.at[side, stage], to_left,
@@ -125,7 +144,7 @@
         )
 
     def detour(side, unit, part, device):
-        number, start, size, turns = unit
+        number, start, size, turns, stage = unit
         span = pl.ds(start, size)
         return remote(
             strips.at[side, part, span], relay.at[part, span],
@@ -133,11 +152,11 @@
         )
 
     def onward(side, unit, part, device):
-        number, start, size, turns = unit
+        number, start, size, turns, stage = unit
         span = pl.ds(start, size)
         return remote(
             relay.at[part, span], arrived.at[1 - side, span, part],
-            relay_sent.at[part, number], strip_sem.at[1 - side, stage_of(start)], device,
+            relay_sent.at[turn(unit, part)], strip_sem.at[1 - side, stage], device,
         )
 
     def turn(unit, part):
@@ -170,16 +189,6 @@
         def _():
             strip(1, unit, part, to_right).start()
 
-    first_units = [
-        (number, start, size, FIRST_TURN[number]) for number, (start, size) in enumerate(FIRST)
-    ]
-
-    def group_unit(g):
-        kinds = len(GROUP_TURN)
-        place = (g - HEAD // GROUP) % kinds
-        turns = tuple(pick(place, [GROUP_TURN[i][part] for i in range(kinds)]) for part in (0, 1))
-        return len(FIRST) - HEAD // GROUP + g, g * GROUP, GROUP, turns
-
     def relays_right(unit, part):
         return even & far_right & by_relay_right(unit, part)
 
@@ -198,15 +207,11 @@
                 detour(0, unit, part, to_right).wait_recv()
                 onward(0, unit, part, to_far_left).start()
 
-    def relay_done(unit):
-        for part in (0, 1):
-            @pl.when(relays_right(unit, part))
-            def _():
-                onward(1, unit, part, to_far_right).wait_send()
-
-            @pl.when(relays_left(unit, part))
-            def _():
-                onward(0, unit, part, to_far_left).wait_send()
+    def relayed(kind):
+        span = pl.ds(0, 2 * count // TURNS)
+        return remote(
+            relay.at[0, span], relay.at[0, span], relay_sent.at[kind], relay_sem.at[0, 0], to_left
+        )
 
     def place_copy(first, size, target, number, device):
         return remote(
@@ -219,13 +224,22 @@
     place_right = place_copy(0, 3, 3, 2, to_right)
     place_left = place_copy(0, 3, 6, 3, to_left)
 
-    def along_rows(slot, k):
-        plane = planes[slot, k]
+    def along_rows(plane, k):
         low = jnp.dot(plane, along[k, :, :half], preferred_element_type=jnp.float32)
         cut = half - RY
         high = jnp.dot(plane[:, cut:], along[k, cut:, half:], preferred_element_type=jnp.float32)
         return low, high
 
+    def mix(now, later, k, number):
+        lanes = slice(number * half, (number + 1) * half)
+        fraction = (shifts_ref[k] // 16 % 4).astype(jnp.float32) * 0.25
+        mixed = now * (1.0 - fraction) + later * fraction
+        held[k, :, lanes] = later
+        top = mixed.astype(jnp.bfloat16)
+        rest = (mixed - top.astype(jnp.float32)).astype(jnp.bfloat16)
+        parts[2 * k * length : (2 * k + 1) * length, lanes] = top
+        parts[(2 * k + 1) * length : (2 * k + 2) * length, lanes] = rest
+
     small = [
         pltpu.make_async_copy(source, target, small_sem.at[number])
         for number, (source, target) in enumerate(
@@ -234,6 +248,8 @@
     ]
     for copy in small:
         copy.start()
+    for n in range(2):
+        fetch(n).start()
     barrier = pltpu.get_barrier_semaphore()
     peers = (
         (has_left, to_left), (has_right, to_right), (has_below, to_below), (has_above, to_above),
@@ -243,10 +259,10 @@
         @pl.when(there)
         def _():
             pl.semaphore_signal(barrier, inc=1, device_id=device, device_id_type=MESH)
-    for n in range(RING):
-        fetch(n).start()
     for copy in small:
         copy.wait()
+    for n in range(2, RING):
+        fetch(n).start()
 
     starts_x = [offsets_ref[0, k] - column * BX for k in range(slots)]
     starts_y = [offsets_ref[1, k] - row * BY for k in range(slots)]
@@ -281,6 +297,13 @@
                 jnp.where(source == target[:, lanes] + 1, after[:, lanes], 0.0),
             )
             along[k, first:, lanes] = blend.astype(jnp.bfloat16)
+    fetch(0).wait()
+    fetch(1).wait()
+    for k in range(slots):
+        both = planes[k, :2].reshape(2 * length, rows)
+        for number, rising in enumerate(along_rows(both, k)):
+            mix(rising[:length], rising[length:], k, number)
+    fetch(RING).start()
     wide = 2 * slots * length
     number = whole_iota((1, wide), 1)
     part = number // length
@@ -298,13 +321,6 @@
     blend = jnp.where(cell == target, here, jnp.where(cell == target - 1, after, 0.0))
     across[...] = blend.astype(jnp.bfloat16)
 
-    fetch(0).wait()
-    for k in range(slots):
-        low, high = along_rows(0, k)
-        held[k, :, :half] = low
-        held[k, :, half:] = high
-    fetch(RING).start()
-
     def merge(n, part, there):
         @pl.when((n >= 0) & (n < count))
         def _():
@@ -321,18 +337,41 @@
                 strips[0, part, n] += edges_in[part, n, :RX]
                 strips[1, part, n] += edges_in[part, n, RX:]
 
-            for unit in first_units:
+            for unit in units:
                 @pl.when(n == unit[1] + unit[2] - 1)
                 def _():
                     send_unit(unit, part)
 
-            @pl.when((n >= HEAD) & (n % GROUP == GROUP - 1))
-            def _():
-                send_unit(group_unit(n // GROUP), part)
-
     lag_near = jnp.where(has_near, LAG_NEAR, 0)
     lag_far = jnp.where(has_far, LAG_FAR, 0)
 
+    def outer(s, left, right):
+        edges[0, s, :RX] = left[:, :RY]
+        edges[0, s, RX:] = right[:, :RY]
+        edges[1, s, :RX] = left[:, RY + BY :]
+        edges[1, s, RX:] = right[:, RY + BY :]
+        for part in (0, 1):
+            strips[0, part, s] = left[:, (part + 1) * RY : (part + 2) * RY]
+            strips[1, part, s] = right[:, (part + 1) * RY : (part + 2) * RY]
+
+    def send_edges(s):
+        @pl.when(has_below)
+        def _():
+            edge_below(s).start()
+
+        @pl.when(has_above)
+        def _():
+            edge_above(s).start()
+
+    def inner(s, centre):
+        middles[0, s] = centre[:, :RY]
+        middles[1, s] = centre[:, RY + BY :]
+        out_ref[s] = centre[:, RY : RY + BY]
+
+    def merges(s):
+        merge(s - lag_near, near, has_near)
+        merge(s - lag_far, far, has_far)
+
     def step(s, carry):
         @pl.when(s < count)
         def _():
@@ -342,65 +381,28 @@
 
             slot = jnp.minimum(s + 1, count - 1) % RING
             for k in range(slots):
-                fraction = (shifts_ref[k] // 16 % 4).astype(jnp.float32) * 0.25
-                for number, later in enumerate(along_rows(slot, k)):
-                    lanes = slice(number * half, (number + 1) * half)
-                    mixed = held[k, :, lanes] * (1.0 - fraction) + later * fraction
-                    held[k, :, lanes] = later
-                    top = mixed.astype(jnp.bfloat16)
-                    rest = (mixed - top.astype(jnp.float32)).astype(jnp.bfloat16)
-                    parts[2 * k * length : (2 * k + 1) * length, lanes] = top
-                    parts[(2 * k + 1) * length : (2 * k + 2) * length, lanes] = rest
+                for number, later in enumerate(along_rows(planes[k, slot], k)):
+                    mix(held[k, :, number * half : (number + 1) * half], later, k, number)
 
             @pl.when(s + 1 + RING < count)
             def _():
                 fetch(s + 1 + RING).start()
 
             total = jnp.dot(across[...], parts[...], preferred_element_type=jnp.float32)
-            left, centre, right = total[:RX], total[RX : RX + BX], total[RX + BX :]
-            edges[0, s, :RX] = left[:, :RY]
-            edges[0, s, RX:] = right[:, :RY]
-            edges[1, s, :RX] = left[:, RY + BY :]
-            edges[1, s, RX:] = right[:, RY + BY :]
-            for part in (0, 1):
-                strips[0, part, s] = left[:, (part + 1) * RY : (part + 2) * RY]
-                strips[1, part, s] = right[:, (part + 1) * RY : (part + 2) * RY]
-
-            @pl.when(s == 0)
-            def _():
-                pl.semaphore_wait(barrier, sum(jnp.where(there, 1, 0) for there, device in peers))
-
-                @pl.when(has_above)
-                def _():
-                    place_above.start()
-
-                @pl.when(has_below)
-                def _():
-                    place_below.start()
-
+            outer(s, total[:RX], total[RX + BX :])
+            send_edges(s)
+            inner(s, total[RX : RX + BX])
+
+        merges(s)
+
+        @pl.when(s == LAG_PLACE)
+        def _():
             @pl.when(has_below)
             def _():
-                edge_below(s).start()
+                place_above.wait_recv()
 
             @pl.when(has_above)
             def _():
-                edge_above(s).start()
-
-            middles[0, s] = centre[:, :RY]
-            middles[1, s] = centre[:, RY + BY :]
-            out_ref[s] = centre[:, RY : RY + BY]
-
-        merge(s - lag_near, near, has_near)
-        merge(s - lag_far, far, has_far)
-
-        @pl.when(s == LAG_PLACE)
-        def _():
-            @pl.when(has_below)
-            def _():
-                place_above.wait_recv()
-
-            @pl.when(has_above)
-            def _():
                 place_below.wait_recv()
 
             @pl.when(has_right)
@@ -413,7 +415,41 @@
 
         return carry
 
-    lax.fori_loop(0, count + max(LAG_NEAR, LAG_FAR), step, 0)
+    total = jnp.dot(across[...], parts[...], preferred_element_type=jnp.float32)
+    outer(0, total[:RX], total[RX + BX :])
+    inner(0, total[RX : RX + BX])
+    pl.semaphore_wait(barrier, sum(jnp.where(there, 1, 0) for there, device in peers))
+    send_edges(0)
+    merges(0)
+
+    @pl.when(has_above)
+    def _():
+        place_above.start()
+
+    @pl.when(has_below)
+    def _():
+        place_below.start()
+
+    fetch(1 + RING).start()
+    lax.fori_loop(1, count + max(LAG_NEAR, LAG_FAR), step, 0)
+
+    for side, there in ((0, has_below), (1, has_above)):
+        @pl.when(jnp.logical_not(there))
+        def _():
+            def clear(n, carry):
+                middles_in[side, n] = jnp.zeros(middles_in.shape[2:], jnp.float32)
+                return carry
+
+            lax.fori_loop(0, count, clear, 0)
+
+    for side, there in ((0, has_left), (1, has_right)):
+        @pl.when(jnp.logical_not(there))
+        def _():
+            def clear(n, carry):
+                arrived[side, n] = jnp.zeros(arrived.shape[2:], jnp.float32)
+                return carry
+
+            lax.fori_loop(0, count, clear, 0)
 
     @pl.when(has_below)
     def _():
@@ -451,14 +487,8 @@
             total += (ramp_at(cell_x - start_x, length) * weight) * ramp_at(cell_y - start_y, rows)
     scale[...] = 1.0 / jnp.maximum(total, 1.0)
 
-    for unit in first_units:
+    for unit in units:
         relay_unit(unit)
-
-    def relay_group(g, carry):
-        relay_unit(group_unit(g))
-        return carry
-
-    lax.fori_loop(HEAD // GROUP, groups, relay_group, 0)
 
     @pl.when(has_below)
     def _():
@@ -472,44 +502,29 @@
         middle(1, to_above).wait_send()
         middle(0, to_below).wait_recv()
 
-    def finish_stage(stage, carry):
+    def finish(n, carry):
+        for part in (0, 1):
+            lanes = slice(part * RY, (part + 1) * RY)
+            for side in (0, 1):
+                cells = slice(side * RX, (side + 1) * RX)
+                total = out_ref[n, cells, lanes] + middles_in[part, n, cells]
+                total += arrived[side, n, part]
+                out_ref[n, cells, lanes] = total * scale[cells, lanes]
+        return carry
+
+    for stage in range(STAGES):
+        inside = [unit for unit in units if unit[4] == stage]
+        first, last = inside[0][1], inside[-1][1] + inside[-1][2]
+
         @pl.when(has_left)
         def _():
-            whole_stage(0, stage).wait_recv()
+            whole_stage(0, stage, first, last).wait_recv()
 
         @pl.when(has_right)
         def _():
-            whole_stage(1, stage).wait_recv()
-
-        def finish(i, carry):
-            n = stage * HEAD + i
-
-            @pl.when(has_below)
-            def _():
-                out_ref[n, :, :RY] += middles_in[0, n]
-
-            @pl.when(has_above)
-            def _():
-                out_ref[n, :, RY:] += middles_in[1, n]
-
-            for part in (0, 1):
-                lanes = slice(part * RY, (part + 1) * RY)
-
-                @pl.when(has_left)
-                def _():
-                    out_ref[n, :RX, lanes] += arrived[0, n, part]
-
-                @pl.when(has_right)
-                def _():
-                    out_ref[n, BX - RX :, lanes] += arrived[1, n, part]
-
-            out_ref[n] = out_ref[n] * scale[...]
-            return carry
-
-        lax.fori_loop(0, HEAD, finish, 0)
-        return carry
-
-    lax.fori_loop(0, count // HEAD, finish_stage, 0)
+            whole_stage(1, stage, first, last).wait_recv()
+
+        lax.fori_loop(first, last, finish, 0)
 
     @pl.when(has_left)
     def _():
@@ -519,20 +534,19 @@
     def _():
         whole_strips(1, to_right).wait_send()
 
-    for unit in first_units:
-        relay_done(unit)
-
-    def relay_group_done(g, carry):
-        relay_done(group_unit(g))
-        return carry
-
-    lax.fori_loop(HEAD // GROUP, groups, relay_group_done, 0)
+    for kind in range(TURNS):
+        right = even & far_right & (kind * pairs < TURNS * (pairs - 1 - pair))
+        left = jnp.logical_not(even) & far_left & (kind * pairs < TURNS * pair)
+
+        @pl.when(right | left)
+        def _():
+            relayed(kind).wait_send()
 
 
 def local(grid_x, grid_y, tiles, tile_offsets, tile_shifts, tile_counts):
     slots, count, length, rows = tiles.shape
     extent_x, extent_y = BX + 2 * RX, BY + 2 * RY
-    units = len(FIRST) + (count - HEAD) // GROUP
+    units = len(units_of(count))
     vmem = lambda *shape: pltpu.VMEM(shape, jnp.float32)
     sems = lambda *shape: pltpu.SemaphoreType.DMA(shape)
     return pl.pallas_call(
@@ -549,7 +563,7 @@
             pltpu.SMEM((2, slots), jnp.int32),
             pltpu.SMEM((slots,), jnp.int32),
             pltpu.SMEM((1, 1), jnp.int32),
-            pltpu.VMEM((RING, slots, length, rows), jnp.bfloat16),
+            pltpu.VMEM((slots, RING, length, rows), jnp.bfloat16),
             vmem(2, 2, count, RX, RY),
             vmem(2, count, 2, RX, RY),
             vmem(2, count, RX, RY),
@@ -564,7 +578,7 @@
             pltpu.VMEM((2 * slots * length, extent_y), jnp.bfloat16),
             vmem(BX, BY),
             sems(3), sems(RING),
-            sems(2), sems(2, count // HEAD), sems(2, units), sems(2, units),
+            sems(2), sems(2, STAGES), sems(TURNS), sems(2, units),
             sems(2), sems(2, FLIGHT),
             sems(2), sems(2),
             sems(4), sems(4),

time: 90.3 us -> 88.7 us (0.982)
  Pallas kernels: 87.3 us -> 85.9 us
    pallas_call x1, Pallas kernels: 87.3 us -> 85.9 us  [local(): pl.pallas_call(functools.partial(kernel, grid_x, grid_y), in_specs=[pl.Bl...]
where the time goes in v2:
time: 88.7 us; the launch traced here: 88.6 us
  Pallas kernels  85.9 us (97%)
  local copies, waits for them, and re-layouts  2.02 us (2%)
    pallas_call x1, Pallas kernels, local(): pl.pallas_call(functools.partial(kernel, grid_x, grid_y), in_specs=[pl.Bl...  85.9 us
    unnamed x1, local copies, waits for them, and re-layouts  2.02 us

profile of v2, /device:TPU:1, one launch (start us, length us, event | category | flops | bytes accessed | tf_op | source)
XLA Modules:
  0.0 88.6 jit_solution(12218297528741965348)
XLA Ops:
  0.7 85.9 %merged.1 = f32[32,128,256]{2,1,0:T(8,128)S(1)} custom-call(s32[2,3]{1,0:T(2,128)} %offsets_hbm.1, s32[3]{0:T(128)} %shifts_hbm.1, s32[1,1]{1,0:T(1,128)} %bitcast.1.counts_hbm, bf16[3,32,192,384]{3,2,1,0:T(8,128)(2,1)} %tiles_ref.1), custom_call_target="tpu_custom_call" | custom-call | tf_op jit(solution)/shard_map/merged/pallas_call | solution.py:552
  86.5 2.0 %copy.6 = f32[32,128,256]{2,1,0:T(8,128)} copy(f32[32,128,256]{2,1,0:T(8,128)S(1)} %merged.1) | data formatting | bytes 8388608

commit v3 on v2

--- a/solution.py
+++ b/solution.py
@@ -15,7 +15,7 @@
 RING = 4
 STEPS = (1, 2)
 LAST = 2
-STAGES = 4
+STAGES = 3
 TURNS = 4
 FLIGHT = 8
 LAG_NEAR = 1
@@ -70,7 +70,7 @@
     grid_x, grid_y, offsets_hbm, shifts_hbm, counts_hbm, tiles_ref, out_ref,
     offsets_ref, shifts_ref, counts_ref,
     planes, strips, arrived, relay, edges, edges_in, middles, middles_in, places,
-    across, along, held, parts, scale,
+    across, along, brims, held, parts, scale,
     small_sem, plane_sem, strip_sent, strip_sem, relay_sent, relay_sem,
     edge_sent, edge_sem, middle_sent, middle_sem, place_sent, place_sem,
 ):
@@ -78,6 +78,7 @@
     extent_x, extent_y = across.shape[0], along.shape[2]
     half = extent_y // 2
     units = units_of(count)
+    turning = [unit for unit in units if min(unit[3]) < TURNS - 1]
     pairs = grid_x // 2
     column, row = lax.axis_index("gx"), lax.axis_index("gy")
     even = column % 2 == 0
@@ -164,12 +165,25 @@
         return jnp.where(part == 0, lower, upper)
 
     def by_relay_left(unit, part):
-        return turn(unit, part) * pairs < TURNS * pair
+        kind = turn(unit, part)
+        return (kind < TURNS - 1) & (kind * pairs < TURNS * pair)
 
     def by_relay_right(unit, part):
-        return turn(unit, part) * pairs < TURNS * (pairs - 1 - pair)
+        kind = turn(unit, part)
+        return (kind < TURNS - 1) & (kind * pairs < TURNS * (pairs - 1 - pair))
 
     def send_unit(unit, part):
+        if min(unit[3]) == TURNS - 1:
+            @pl.when(has_left)
+            def _():
+                strip(0, unit, part, to_left).start()
+
+            @pl.when(has_right)
+            def _():
+                strip(1, unit, part, to_right).start()
+
+            return
+
         turns_left = even & by_relay_left(unit, part)
         turns_right = jnp.logical_not(even) & by_relay_right(unit, part)
 
@@ -225,9 +239,12 @@
     place_left = place_copy(0, 3, 6, 3, to_left)
 
     def along_rows(plane, k):
-        low = jnp.dot(plane, along[k, :, :half], preferred_element_type=jnp.float32)
+        low = jnp.dot(plane[:, :half], along[k, :half, :half], preferred_element_type=jnp.float32)
         cut = half - RY
         high = jnp.dot(plane[:, cut:], along[k, cut:, half:], preferred_element_type=jnp.float32)
+        beyond = pltpu.roll(plane[:, half : half + LANES].astype(jnp.float32), LANES - 1, 1)
+        beyond = beyond * brims[k, 0:1, :]
+        low = jnp.concatenate([low[:, : half - LANES], low[:, half - LANES :] + beyond], axis=1)
         return low, high
 
     def mix(now, later, k, number):
@@ -290,13 +307,17 @@
         ramp = ramp_at(target, rows)
         here = jnp.where(target == rows - 1, ramp, ramp * (1.0 - fraction))
         after = ramp * fraction
-        for first, lanes in ((0, slice(0, half)), (half - RY, slice(half, extent_y))):
-            source = whole_iota((rows - first, half), 0) + first
+        edge = slice(half - LANES, half)
+        brim = jnp.where(target[:, edge] == half - 1, after[:, edge], 0.0)
+        brim = jnp.where(whole_iota((1, LANES), 1) == LANES - 1, brim, 0.0)
+        brims[k] = jnp.broadcast_to(brim, brims.shape[1:])
+        for first, last, lanes in ((0, half, slice(0, half)), (half - RY, rows, slice(half, extent_y))):
+            source = whole_iota((last - first, half), 0) + first
             blend = jnp.where(
                 source == target[:, lanes], here[:, lanes],
                 jnp.where(source == target[:, lanes] + 1, after[:, lanes], 0.0),
             )
-            along[k, first:, lanes] = blend.astype(jnp.bfloat16)
+            along[k, first:last, lanes] = blend.astype(jnp.bfloat16)
     fetch(0).wait()
     fetch(1).wait()
     for k in range(slots):
@@ -487,7 +508,7 @@
             total += (ramp_at(cell_x - start_x, length) * weight) * ramp_at(cell_y - start_y, rows)
     scale[...] = 1.0 / jnp.maximum(total, 1.0)
 
-    for unit in units:
+    for unit in turning:
         relay_unit(unit)
 
     @pl.when(has_below)
@@ -534,7 +555,7 @@
     def _():
         whole_strips(1, to_right).wait_send()
 
-    for kind in range(TURNS):
+    for kind in range(TURNS - 1):
         right = even & far_right & (kind * pairs < TURNS * (pairs - 1 - pair))
         left = jnp.logical_not(even) & far_left & (kind * pairs < TURNS * pair)
 
@@ -546,7 +567,7 @@
 def local(grid_x, grid_y, tiles, tile_offsets, tile_shifts, tile_counts):
     slots, count, length, rows = tiles.shape
     extent_x, extent_y = BX + 2 * RX, BY + 2 * RY
-    units = len(units_of(count))
+    turning = sum(min(unit[3]) < TURNS - 1 for unit in units_of(count))
     vmem = lambda *shape: pltpu.VMEM(shape, jnp.float32)
     sems = lambda *shape: pltpu.SemaphoreType.DMA(shape)
     return pl.pallas_call(
@@ -574,11 +595,12 @@
             vmem(9, 8 * pl.cdiv(slots, 8), LANES),
             pltpu.VMEM((extent_x, 2 * slots * length), jnp.bfloat16),
             pltpu.VMEM((slots, rows, extent_y), jnp.bfloat16),
+            vmem(slots, 8, LANES),
             vmem(slots, length, extent_y),
             pltpu.VMEM((2 * slots * length, extent_y), jnp.bfloat16),
             vmem(BX, BY),
             sems(3), sems(RING),
-            sems(2), sems(2, STAGES), sems(TURNS), sems(2, units),
+            sems(2), sems(2, STAGES), sems(TURNS - 1), sems(2, turning),
             sems(2), sems(2, FLIGHT),
             sems(2), sems(2),
             sems(4), sems(4),

time: 88.7 us -> 88.6 us (level)
  no operation moved by 1% of the time
where the time goes in v3:
time: 88.6 us; the launch traced here: 88.5 us
  Pallas kernels  85.8 us (97%)
  local copies, waits for them, and re-layouts  2.02 us (2%)
    pallas_call x1, Pallas kernels, local(): pl.pallas_call(functools.partial(kernel, grid_x, grid_y), in_specs=[pl.Bl...  85.8 us
    unnamed x1, local copies, waits for them, and re-layouts  2.02 us

profile of v3, /device:TPU:1, one launch (start us, length us, event | category | flops | bytes accessed | tf_op | source)
XLA Modules:
  0.0 88.5 jit_solution(1535817901957140734)
XLA Ops:
  0.7 85.8 %merged.1 = f32[32,128,256]{2,1,0:T(8,128)S(1)} custom-call(s32[2,3]{1,0:T(2,128)} %offsets_hbm.1, s32[3]{0:T(128)} %shifts_hbm.1, s32[1,1]{1,0:T(1,128)} %bitcast.1.counts_hbm, bf16[3,32,192,384]{3,2,1,0:T(8,128)(2,1)} %tiles_ref.1), custom_call_target="tpu_custom_call" | custom-call | tf_op jit(solution)/shard_map/merged/pallas_call | solution.py:573
  86.4 2.0 %copy.6 = f32[32,128,256]{2,1,0:T(8,128)} copy(f32[32,128,256]{2,1,0:T(8,128)S(1)} %merged.1) | data formatting | bytes 8388608
